TPU v7x, 512 devices: a 4x2x32 block of a 4x8x32 slice. The times are simulated.
512 devices in a mesh: groups: 2 (over y), tm: 32 (over z), height: 8 (over x, core).
Axes of the slice: x: 4, y: 2, z: 32, core: 2. Of those that a mesh axis runs over, the one named last changes fastest.
The devices are a block of a 4x8x32 slice.
Arguments:
- video: bfloat16 [128, 32, 64, 256], P(('groups', 'tm'), 'height'), parts along dimension 0, may hold values from -8 to 8
- norm_gain: float32 [256], replicated, may hold values from 0.25 to 1.75
- spatial_weight: bfloat16 [3, 3, 256, 256], P(None, None, 'height'), may hold values from -0.125 to 0.125
- temporal_weight: bfloat16 [3, 256, 256], replicated, may hold values from -0.21875 to 0.21875
- haar_weight: bfloat16 [2048, 512], replicated, may hold values from -0.125 to 0.125
- query_weight: bfloat16 [512, 512], replicated, may hold values from -1.5 to 1.5
- key_weight: bfloat16 [512, 512], replicated, may hold values from -1.5 to 1.5
Outputs:
- encoded: bfloat16 [64, 16, 32, 512], P(('groups', 'tm'), 'height'), parts along dimension 0
There are 2 independent parts, one for each index of `groups`. A program takes and returns all parts, laid end to end along the dimension named above; an argument that names none is the same for every part. Nothing has to cross between parts.
All inputs are finite; a program needn't handle non-finite values.
Results may differ from a plain program's by a relative error of at most 0.015.
Values may be sent and summed in bfloat16 or wider, within the bound.
No kernel may reach another device: no remote copies, remote signals or barrier semaphores. Data moves between devices by JAX's collectives and lax.ppermute only.
A program may use at most 64 MiB of HBM per device.

v0:
```python
import jax
import jax.numpy as jnp
from jax import lax
from jax.sharding import PartitionSpec as P

HEAD_DIM = 64


epsilon = 1e-06
inv_root = 0.7071067811865476


def extended_2(x, sides, width):
    for axis, dim in sides:
        devices, length = (lax.axis_size(axis), x.shape[dim])
        up = [(i, (i + 1) % devices) for i in range(devices - 1)]
        down = [(j, i) for i, j in up]
        last = lax.slice_in_dim(x, length - width, length, axis=dim)
        initial = lax.slice_in_dim(x, 0, width, axis=dim)
        before = lax.ppermute(last, axis, up)
        after = lax.ppermute(initial, axis, down)
        x = jnp.concatenate([before, x, after], axis=dim)
    return x


def laid_out(pieces, dim):
    pieces = jnp.moveaxis(pieces, 0, dim)
    shape = pieces.shape
    return pieces.reshape(*shape[:dim], shape[dim] * shape[dim + 1], *shape[dim + 2 :])


def from_everyone(x, axis):
    copies = jnp.broadcast_to(x, (lax.axis_size(axis), *x.shape))
    return lax.all_to_all(copies, axis, split_axis=0, concat_axis=0, tiled=True)


def gathered_copies(x, axis, dim):
    return laid_out(from_everyone(x, axis), dim)


def shifted(x, axis, by):
    devices = lax.axis_size(axis)
    pairs = [(i, i + by) for i in range(devices) if 0 <= i + by < devices]
    return lax.ppermute(x, axis, pairs)


def activate(video, norm_gain):
    values = video.astype(jnp.float32)
    square = jnp.mean(values * values, axis=-1, keepdims=True)
    normed = values * lax.rsqrt(square + epsilon) * norm_gain
    return (normed * jax.nn.sigmoid(normed)).astype(jnp.bfloat16)


def haar_split(values, axis_pos):
    first = lax.index_in_dim(values, 0, axis_pos, keepdims=False)
    second = lax.index_in_dim(values, 1, axis_pos, keepdims=False)
    return jnp.stack([first + second, first - second], axis=axis_pos) * inv_root


def haar_bands(merged):
    frames, rows, columns, channels = merged.shape
    values = merged.astype(jnp.float32).reshape(
        frames // 2, 2, rows // 2, 2, columns // 2, 2, channels
    )
    for axis_pos in (1, 3, 5):
        values = haar_split(values, axis_pos)
    values = jnp.transpose(values, (0, 2, 4, 1, 3, 5, 6))
    return values.reshape(frames // 2, rows // 2, columns // 2, 8 * channels).astype(jnp.bfloat16)


def causal_attention(parts):
    queries, keys, values = parts
    frames, places, width = queries.shape
    heads = width // HEAD_DIM
    query_heads = queries.reshape(frames, places, heads, HEAD_DIM)
    key_heads = keys.reshape(frames, places, heads, HEAD_DIM)
    value_heads = values.reshape(frames, places, heads, HEAD_DIM)
    scores = jnp.einsum(
        "tphd,sphd->phts", query_heads, key_heads, preferred_element_type=jnp.float32
    ) * HEAD_DIM ** (-0.5)
    order = jnp.arange(frames)
    allowed = order[None, :] <= order[:, None]
    scores = jnp.where(allowed, scores, -1e30)
    top = jnp.max(scores, axis=-1, keepdims=True)
    weights = jnp.exp(scores - top)
    probs = (weights / jnp.sum(weights, axis=-1, keepdims=True)).astype(jnp.bfloat16)
    mixed = jnp.einsum("phts,sphd->tphd", probs, value_heads, preferred_element_type=jnp.float32)
    return mixed.reshape(frames, places, width).astype(jnp.bfloat16)


def body(video, norm_gain, spatial_weight, temporal_weight, haar_weight, query_weight, key_weight):
    frames, rows, columns, channels = video.shape
    outward = spatial_weight.shape[3]
    acted = activate(video, norm_gain)
    rimmed = extended_2(acted, (("height", 1),), 1)
    padded = jnp.pad(rimmed, ((0, 0), (0, 0), (1, 1), (0, 0)))
    start_total = jnp.zeros((frames * rows * columns, outward), jnp.float32)
    total = start_total
    piece = gathered_copies(spatial_weight, "height", 2)
    count = piece.shape[2]
    for row_tap in range(3):
        for col_tap in range(3):
            add_window = padded[
                :, row_tap : row_tap + rows, col_tap : col_tap + columns, :
            ].reshape(-1, count)
            total = total + jnp.dot(
                add_window, piece[row_tap, col_tap], preferred_element_type=jnp.float32
            )
    spatial = total.astype(jnp.bfloat16).reshape(frames, rows, columns, outward)
    earlier = shifted(spatial, "tm", 1)
    extended = jnp.concatenate([earlier, spatial], axis=0)
    temporal = jnp.zeros((frames * rows * columns, channels), jnp.float32)
    for frame_tap in range(3):
        window = extended[frame_tap : frame_tap + frames].reshape(-1, outward)
        temporal = temporal + jnp.dot(
            window, temporal_weight[frame_tap], preferred_element_type=jnp.float32
        )
    merged = (video.astype(jnp.float32).reshape(-1, channels) + temporal).astype(jnp.bfloat16)
    bands = haar_bands(merged.reshape(frames, rows, columns, channels))
    coarse_frames, coarse_rows, coarse_cols, band_width = bands.shape
    latent = jnp.dot(
        bands.reshape(-1, band_width), haar_weight, preferred_element_type=jnp.float32
    ).astype(jnp.bfloat16)
    width = latent.shape[1]
    places = coarse_rows * coarse_cols
    latent_three = latent.reshape(coarse_frames, places, width)
    members = lax.axis_size("tm")
    per_group = places // members
    grouped = latent_three.reshape(coarse_frames, members, per_group, width)
    gathered = lax.all_to_all(grouped, "tm", split_axis=1, concat_axis=0, tiled=True)
    all_frames, single, count, depth = gathered.shape
    flat_latent = gathered.reshape(-1, depth)
    group_queries = jnp.dot(flat_latent, query_weight, preferred_element_type=jnp.float32).astype(
        jnp.bfloat16
    )
    group_keys = jnp.dot(flat_latent, key_weight, preferred_element_type=jnp.float32).astype(
        jnp.bfloat16
    )
    shaped = tuple(
        (
            item.reshape(all_frames, single * count, depth)
            for item in (group_queries, group_keys, flat_latent)
        )
    )
    mixed_group = causal_attention(shaped)
    regrouped = mixed_group.reshape(all_frames, single, count, depth)
    returned = lax.all_to_all(regrouped, "tm", split_axis=0, concat_axis=1, tiled=True)
    mixed = returned.reshape(coarse_frames, places, width)
    result = (latent_three.astype(jnp.float32) + mixed.astype(jnp.float32)).astype(jnp.bfloat16)
    return result.reshape(coarse_frames, coarse_rows, coarse_cols, width)


def solution(mesh):
    in_specs = (
        P(("groups", "tm"), "height", None, None),
        P(),
        P(None, None, "height", None),
        P(),
        P(),
        P(),
        P(),
    )
    out_specs = P(("groups", "tm"), "height", None, None)
    return jax.shard_map(body, mesh=mesh, in_specs=in_specs, out_specs=out_specs, check_vma=False)
```

profile of v0, /device:TPU:40, one launch (start us, length us, event | category | flops | bytes accessed | tf_op | source)
XLA Modules:
  0.0 146.4 jit_solution(16923401958046840282)
XLA Ops:
  0.0 2.2 %broadcast_in_dim.10 = bf16[8,3,3,32,256]{4,3,2,1,0:T(8,128)(2,1)} broadcast(bf16[3,3,32,256]{3,2,1,0:T(8,128)(2,1)} %param.9), dimensions={1,2,3,4} | broadcast | bytes 1327104 | tf_op jit(solution)/shard_map/broadcast_in_dim | solution.py:33
  2.3 4.7 %all-to-all-start = ((bf16[8,3,3,32,256]{4,3,2,1,0:T(8,128)(2,1)}), bf16[8,3,3,32,256]{4,3,2,1,0:T(8,128)(2,1)S(1)}, u32[]{:S(2)}, u32[]{:S(2)}) async-start(bf16[8,3,3,32,256]{4,3,2,1,0:T(8,128)(2,1)} %broadcast_in_dim.10), calls=%async_computation | async-start | bytes 2359296 | tf_op jit(solution)/shard_map/all_to_all | solution.py:34
  7.1 1.2 multiply_convert_fusion
  8.4 2.4 %collective-permute-start = (bf16[2,1,64,256]{3,2,1,0:T(8,128)(2,1)S(1)}, bf16[2,1,64,256]{3,2,1,0:T(8,128)(2,1)S(1)}, u32[]{:S(2)}, u32[]{:S(2)}) collective-permute-start(bf16[2,1,64,256]{3,2,1,0:T(8,128)(2,1)S(1)} %get-tuple-element.21), channel_id=1, source_target_pairs={{0,1},{1,2},{2,3},{3,4},{4,5},{5,6},{6,7},{8,9},{9,10},{10,11},{11... | collective-permute-start | bytes 196616 | tf_op jit(solution)/shard_map/ppermute | solution.py:20
  10.8 1.3 collective-permute-start.1
  12.1 3.0 %collective-permute-done.1 = bf16[2,1,64,256]{3,2,1,0:T(8,128)(2,1)S(1)} collective-permute-done((bf16[2,1,64,256]{3,2,1,0:T(8,128)(2,1)S(1)}, bf16[2,1,64,256]{3,2,1,0:T(8,128)(2,1)S(1)}, u32[]{:S(2)}, u32[]{:S(2)}) %collective-permute-start.1) | collective-permute-done | bytes 65568 | tf_op jit(solution)/shard_map/ppermute | solution.py:21
  15.2 0.9 pad_maximum_fusion.1
  16.1 1.2 fusion.35
  17.3 7.6 %all-to-all-done = bf16[8,3,3,32,256]{4,3,2,1,0:T(8,128)(2,1)S(1)} async-done(((bf16[8,3,3,32,256]{4,3,2,1,0:T(8,128)(2,1)}), bf16[8,3,3,32,256]{4,3,2,1,0:T(8,128)(2,1)S(1)}, u32[]{:S(2)}, u32[]{:S(2)}) %all-to-all-start) | async-done | bytes 1179680 | tf_op jit(solution)/shard_map/all_to_all | solution.py:34
  25.0 0.8 copy-done.4
  26.6 0.5 copy-done.10
  27.8 0.5 copy-done.7
  28.7 0.5 copy-done.5
  29.5 4.9 %collective-permute-start.2 = (bf16[2,4,64,256]{3,2,1,0:T(8,128)(2,1)S(1)}, bf16[2,4,64,256]{3,2,1,0:T(8,128)(2,1)S(1)}, u32[]{:S(2)}, u32[]{:S(2)}) collective-permute-start(bf16[2,4,64,256]{3,2,1,0:T(8,128)(2,1)S(1)} %bitcast.96), channel_id=1, source_target_pairs={{0,8},{8,16},{16,24},{24,32},{32,40},{40,48},{48,56},{56,64},{64,7... | collective-permute-start | bytes 786440 | tf_op jit(solution)/shard_map/ppermute | solution.py:44
  34.6 6.4 %collective-permute-done.2 = bf16[2,4,64,256]{3,2,1,0:T(8,128)(2,1)S(1)} collective-permute-done((bf16[2,4,64,256]{3,2,1,0:T(8,128)(2,1)S(1)}, bf16[2,4,64,256]{3,2,1,0:T(8,128)(2,1)S(1)}, u32[]{:S(2)}, u32[]{:S(2)}) %collective-permute-start.2) | collective-permute-done | bytes 262176 | tf_op jit(solution)/shard_map/ppermute | solution.py:44
  42.7 0.3 maximum_multiply_fusion.1
  43.0 0.4 slice_add_fusion.1
  43.4 0.6 fusion.18
  44.2 0.5 convolution_convert_fusion.3
  44.7 0.7 reshape_reshape.9
  45.4 45.4 %all-to-all-start.1 = ((bf16[1,32,2,512]{3,2,0,1:T(2,128)(2,1)}), bf16[1,32,2,512]{3,2,0,1:T(2,128)(2,1)S(1)}, u32[]{:S(2)}, u32[]{:S(2)}) async-start(bf16[1,32,2,512]{3,2,0,1:T(2,128)(2,1)} %bitcast.29), calls=%async_computation.1 | async-start | bytes 131072 | tf_op jit(solution)/shard_map/all_to_all | solution.py:130
  90.8 25.4 %all-to-all-done.1 = bf16[1,32,2,512]{3,2,0,1:T(2,128)(2,1)S(1)} async-done(((bf16[1,32,2,512]{3,2,0,1:T(2,128)(2,1)}), bf16[1,32,2,512]{3,2,0,1:T(2,128)(2,1)S(1)}, u32[]{:S(2)}, u32[]{:S(2)}) %all-to-all-start.1) | async-done | bytes 65568 | tf_op jit(solution)/shard_map/all_to_all | solution.py:130
  117.9 27.9 %all_to_all.23 = bf16[32,1,2,512]{3,2,1,0:T(2,128)(2,1)S(1)} all-to-all(bf16[32,1,2,512]{3,2,1,0:T(2,128)(2,1)S(1)} %reshape.246), channel_id=1, replica_groups=mesh['groups'=2,'tm'=32,'height'=8] {'tm'}, dimensions={0} | all-to-all | bytes 131072 | tf_op jit(solution)/shard_map/all_to_all | solution.py:147
  145.8 0.6 add_convert_fusion
  (64 shorter events, 6.2 us)
Async XLA Ops:
  0.0 44.2 %copy-start = (bf16[2048,512]{1,0:T(8,128)(2,1)S(1)}, bf16[2048,512]{1,0:T(8,128)(2,1)}, u32[]{:S(2)}) copy-start(bf16[2048,512]{1,0:T(8,128)(2,1)} %param.11) | copy-start | bytes 6291460
  2.2 4.7 %copy-start.1 = (bf16[2,4,64,256]{3,2,1,0:T(8,128)(2,1)S(1)}, bf16[2,4,64,256]{3,2,1,0:T(8,128)(2,1)}, u32[]{:S(2)}) copy-start(bf16[2,4,64,256]{3,2,1,0:T(8,128)(2,1)} %param.7) | copy-start | bytes 786436
  2.3 4.9 %copy-start.14 = (f32[256]{0:T(256)S(1)}, f32[256]{0:T(256)}, u32[]{:S(2)}) copy-start(f32[256]{0:T(256)} %param.8) | copy-start | bytes 3076
  2.3 22.6 %all-to-all-start = ((bf16[8,3,3,32,256]{4,3,2,1,0:T(8,128)(2,1)}), bf16[8,3,3,32,256]{4,3,2,1,0:T(8,128)(2,1)S(1)}, u32[]{:S(2)}, u32[]{:S(2)}) async-start(bf16[8,3,3,32,256]{4,3,2,1,0:T(8,128)(2,1)} %broadcast_in_dim.10), calls=%async_computation | async-start | bytes 2359296 | tf_op jit(solution)/shard_map/all_to_all | solution.py:34
  8.4 3.8 %collective-permute-start = (bf16[2,1,64,256]{3,2,1,0:T(8,128)(2,1)S(1)}, bf16[2,1,64,256]{3,2,1,0:T(8,128)(2,1)S(1)}, u32[]{:S(2)}, u32[]{:S(2)}) collective-permute-start(bf16[2,1,64,256]{3,2,1,0:T(8,128)(2,1)S(1)} %get-tuple-element.21), channel_id=1, source_target_pairs={{0,1},{1,2},{2,3},{3,4},{4,5},{5,6},{6,7},{8,9},{9,10},{10,11},{11... | collective-permute-start | bytes 196616 | tf_op jit(solution)/shard_map/ppermute | solution.py:20
  10.8 4.3 %collective-permute-start.1 = (bf16[2,1,64,256]{3,2,1,0:T(8,128)(2,1)S(1)}, bf16[2,1,64,256]{3,2,1,0:T(8,128)(2,1)S(1)}, u32[]{:S(2)}, u32[]{:S(2)}) collective-permute-start(bf16[2,1,64,256]{3,2,1,0:T(8,128)(2,1)S(1)} %get-tuple-element.22), channel_id=1, source_target_pairs={{1,0},{2,1},{3,2},{4,3},{5,4},{6,5},{7,6},{9,8},{10,9},{11,10},{12... | collective-permute-start | bytes 196616 | tf_op jit(solution)/shard_map/ppermute | solution.py:21
  24.9 1.0 copy-start.4
  24.9 1.2 copy-start.3
  25.0 1.3 copy-start.8
  26.1 1.0 copy-start.10
  26.3 1.0 copy-start.9
  27.3 0.9 copy-start.7
  27.5 1.0 copy-start.6
  28.2 1.0 copy-start.5
  28.7 5.6 %copy-start.13 = (bf16[3,256,256]{2,1,0:T(8,128)(2,1)S(1)}, bf16[3,256,256]{2,1,0:T(8,128)(2,1)}, u32[]{:S(2)}) copy-start(bf16[3,256,256]{2,1,0:T(8,128)(2,1)} %param.10) | copy-start | bytes 1179652
  29.4 11.8 %copy-start.2 = (bf16[2,4,64,256]{3,2,1,0:T(8,128)(2,1)S(1)}, bf16[2,4,64,256]{3,2,1,0:T(8,128)(2,1)}, u32[]{:S(2)}) copy-start(bf16[2,4,64,256]{3,2,1,0:T(8,128)(2,1)} %param.7) | copy-start | bytes 786436
  29.5 11.5 %collective-permute-start.2 = (bf16[2,4,64,256]{3,2,1,0:T(8,128)(2,1)S(1)}, bf16[2,4,64,256]{3,2,1,0:T(8,128)(2,1)S(1)}, u32[]{:S(2)}, u32[]{:S(2)}) collective-permute-start(bf16[2,4,64,256]{3,2,1,0:T(8,128)(2,1)S(1)} %bitcast.96), channel_id=1, source_target_pairs={{0,8},{8,16},{16,24},{24,32},{32,40},{40,48},{48,56},{56,64},{64,7... | collective-permute-start | bytes 786440 | tf_op jit(solution)/shard_map/ppermute | solution.py:44
  44.2 72.1 %copy-start.11 = (bf16[512,512]{1,0:T(8,128)(2,1)S(1)}, bf16[512,512]{1,0:T(8,128)(2,1)}, u32[]{:S(2)}) copy-start(bf16[512,512]{1,0:T(8,128)(2,1)} %param.12) | copy-start | bytes 1572868
  44.7 72.0 %copy-start.12 = (bf16[512,512]{1,0:T(8,128)(2,1)S(1)}, bf16[512,512]{1,0:T(8,128)(2,1)}, u32[]{:S(2)}) copy-start(bf16[512,512]{1,0:T(8,128)(2,1)} %param.13) | copy-start | bytes 1572868
  45.4 70.9 %all-to-all-start.1 = ((bf16[1,32,2,512]{3,2,0,1:T(2,128)(2,1)}), bf16[1,32,2,512]{3,2,0,1:T(2,128)(2,1)S(1)}, u32[]{:S(2)}, u32[]{:S(2)}) async-start(bf16[1,32,2,512]{3,2,0,1:T(2,128)(2,1)} %bitcast.29), calls=%async_computation.1 | async-start | bytes 131072 | tf_op jit(solution)/shard_map/all_to_all | solution.py:130
where the time goes:
time: 147 us; the launch traced here: 146 us
  starting transfers between devices  58.8 us (40%)
  waiting for transfers between devices  42.4 us (29%)
  blocking collectives  27.9 us (19%)
  local copies, waits for them, and re-layouts  7.88 us (5%)
  other arithmetic  5.04 us (3%)
  matrix products  4.02 us (3%)
    all_to_all x1, starting transfers between devices, body(): lax.all_to_all(grouped, 'tm', split_axis=1, concat_axis=0, tiled=True)  45.4 us
    all_to_all x1, blocking collectives, body(): lax.all_to_all(regrouped, 'tm', split_axis=0, concat_axis=1, tiled=True)  27.9 us
    all_to_all x1, waiting for transfers between devices, body(): lax.all_to_all(grouped, 'tm', split_axis=1, concat_axis=0, tiled=True)  25.4 us
    all_to_all x1, waiting for transfers between devices, from_everyone(): return lax.all_to_all(copies, axis, split_axis=0, concat_axis=0, tiled=True)  7.58 us
    ppermute x1, waiting for transfers between devices, shifted(): return lax.ppermute(x, axis, pairs)  6.42 us
    ppermute x1, starting transfers between devices, shifted(): return lax.ppermute(x, axis, pairs)  4.86 us
    all_to_all x1, starting transfers between devices, from_everyone(): return lax.all_to_all(copies, axis, split_axis=0, concat_axis=0, tiled=True)  4.72 us
    ppermute x1, waiting for transfers between devices, extended_2(): after = lax.ppermute(initial, axis, down)  2.99 us
  transfers between devices with their start and end apart: 5, of which 4 were waited for; matrix products, arithmetic and copies ran while one was open for 3% of the time, Pallas kernels for 0%

commit v1 on v0

v1 whole, which is shorter than its diff:
```python
import jax
import jax.numpy as jnp
from jax import lax
from jax.experimental import pallas as pl
from jax.experimental.pallas import tpu as pltpu
from jax.sharding import PartitionSpec as P

HEAD_DIM = 64
CORES = 2

epsilon = 1e-06
inv_root = 0.7071067811865476

F32 = jnp.float32
BF16 = jnp.bfloat16


def dot(a, b):
    return jnp.dot(a, b, preferred_element_type=F32)


def vmem(count):
    return [pl.BlockSpec(memory_space=pltpu.VMEM) for _ in range(count)]


def params(mib=20):
    return pltpu.CompilerParams(vmem_limit_bytes=mib * 2**20)


def cost(flops, nbytes):
    return pl.CostEstimate(flops=flops, bytes_accessed=nbytes, transcendentals=0)


def prepare_kernel(video_ref, above_ref, below_ref, gain_ref, windows_ref, ordered_ref):
    frames, rows, columns, channels = video_ref.shape
    half = columns // 2
    place = lax.broadcasted_iota(jnp.int32, (3 * columns, columns), 0)
    source = lax.broadcasted_iota(jnp.int32, (3 * columns, columns), 1)
    tap, within = place // columns, place % columns
    wanted = 2 * (within % half) + within // half + tap - 1
    pick = (source == wanted).astype(F32).astype(BF16)
    gain = gain_ref[...]
    for frame in range(frames):
        for row in range(rows + 2):
            if row == 0:
                block = above_ref[frame, 0]
            elif row == rows + 1:
                block = below_ref[frame, 0]
            else:
                block = video_ref[frame, row - 1]
                ordered_ref[frame, row - 1] = dot(pick[columns : 2 * columns], block).astype(BF16)
            values = block.astype(F32)
            square = jnp.mean(values * values, axis=-1, keepdims=True)
            normed = values * lax.rsqrt(square + epsilon) * gain
            acted = (normed * jax.nn.sigmoid(normed)).astype(BF16)
            moved = dot(pick, acted).astype(BF16)
            for t in range(3):
                windows_ref[t, frame, row] = moved[t * columns : (t + 1) * columns]


def haar_rows(values, rows, half):
    out = []
    for pair in range(rows // 2):
        blocks = [
            values[f][((2 * pair + r) * 2 + c) * half : ((2 * pair + r) * 2 + c + 1) * half]
            for f in range(2)
            for r in range(2)
            for c in range(2)
        ]
        for step in (4, 2, 1):
            split = list(blocks)
            for i in range(8):
                if not i & step:
                    split[i] = (blocks[i] + blocks[i + step]) * inv_root
                    split[i + step] = (blocks[i] - blocks[i + step]) * inv_root
            blocks = split
        out.append(jnp.concatenate([b.astype(BF16) for b in blocks], axis=1))
    return jnp.concatenate(out, axis=0)


def spatial_kernel(core_ref, own_ref, other_ref, windows_ref, temporal_ref, haar_ref, spatial_ref, next_ref):
    frames, rows, columns, channels = spatial_ref.shape
    chips = own_ref.shape[0]
    first = core_ref[0] == 0
    taps = []
    for tap in range(9):
        parts = []
        for chip in range(chips):
            own, other = own_ref[chip, tap], other_ref[chip, tap]
            parts += [jnp.where(first, own, other), jnp.where(first, other, own)]
        taps.append(jnp.concatenate(parts, axis=0))
    spatial = []
    for frame in range(frames):
        total = None
        for tap in range(9):
            a, b = tap // 3, tap % 3
            window = windows_ref[b, frame, a : a + rows].reshape(rows * columns, channels)
            term = dot(window, taps[tap])
            total = term if total is None else total + term
        spatial.append(total.astype(BF16))
        spatial_ref[frame] = spatial[-1].reshape(rows, columns, channels)
    early = dot(spatial[0], temporal_ref[0]) + dot(spatial[1], temporal_ref[1])
    late = dot(spatial[1], temporal_ref[0])
    bands = haar_rows([early, late], rows, columns // 2)
    next_ref[...] = dot(bands, haar_ref[...]).astype(BF16)


def latent_kernel(spatial_ref, video_ref, temporal_ref, haar_ref, latent_ref):
    frames, rows, columns, channels = spatial_ref.shape
    first = spatial_ref[0].reshape(rows * columns, channels)
    second = spatial_ref[1].reshape(rows * columns, channels)
    merged = [
        video_ref[0].reshape(rows * columns, channels).astype(F32) + dot(first, temporal_ref[2]),
        video_ref[1].reshape(rows * columns, channels).astype(F32)
        + dot(first, temporal_ref[1])
        + dot(second, temporal_ref[2]),
    ]
    bands = haar_rows(merged, rows, columns // 2)
    latent_ref[...] = dot(bands, haar_ref[...])


def attention_kernel(latent_ref, query_ref, key_ref, out_ref):
    frames = latent_ref.shape[0]
    width = query_ref.shape[0]
    places = latent_ref.shape[1] // width
    rows = places * frames
    latent = jnp.concatenate([latent_ref[:, p * width : (p + 1) * width] for p in range(places)], axis=0)
    queries = dot(latent, query_ref[...]).astype(BF16)
    keys = dot(latent, key_ref[...]).astype(BF16)
    at = lax.broadcasted_iota(jnp.int32, (rows, rows), 0)
    to = lax.broadcasted_iota(jnp.int32, (rows, rows), 1)
    allowed = (at // frames == to // frames) & (to <= at)
    pair = 2 * HEAD_DIM
    lane = lax.broadcasted_iota(jnp.int32, (rows, pair), 1)
    sides = [(lane // HEAD_DIM == i).astype(F32).astype(BF16) for i in range(2)]
    pieces = []
    for start in range(0, width, pair):
        q, k, v = (item[:, start : start + pair] for item in (queries, keys, latent))
        mixed = None
        for side in sides:
            scores = lax.dot_general(q, k * side, (((1,), (1,)), ((), ())), preferred_element_type=F32)
            scores = jnp.where(allowed, scores * HEAD_DIM ** (-0.5), -1e30)
            weights = jnp.exp(scores - jnp.max(scores, axis=-1, keepdims=True))
            probs = (weights / jnp.sum(weights, axis=-1, keepdims=True)).astype(BF16)
            term = dot(probs, v * side)
            mixed = term if mixed is None else mixed + term
        pieces.append((v.astype(F32) + mixed.astype(BF16).astype(F32)).astype(BF16))
    encoded = jnp.concatenate(pieces, axis=1)
    for p in range(places):
        out_ref[:, p * width : (p + 1) * width] = encoded[p * frames : (p + 1) * frames]


def body(video, norm_gain, spatial_weight, temporal_weight, haar_weight, query_weight, key_weight):
    frames, rows, columns, channels = video.shape
    outward = spatial_weight.shape[3]
    width = haar_weight.shape[1]
    height = lax.axis_size("height")
    members = lax.axis_size("tm")
    chips = height // CORES
    slice_depth = spatial_weight.shape[2]

    slices = spatial_weight.reshape(9, slice_depth, outward)
    same_core = [[c + CORES * i for i in range(chips)] for c in range(CORES)]
    own = lax.all_to_all(
        jnp.broadcast_to(slices, (chips, *slices.shape)),
        "height",
        split_axis=0,
        concat_axis=0,
        axis_index_groups=same_core,
        tiled=True,
    )

    above = lax.ppermute(video[:, rows - 1 :], "height", [(i, i + 1) for i in range(height - 1)])
    below = lax.ppermute(video[:, :1], "height", [(i + 1, i) for i in range(height - 1)])
    windows, ordered = pl.pallas_call(
        prepare_kernel,
        out_shape=(
            jax.ShapeDtypeStruct((3, frames, rows + 2, columns, channels), BF16),
            jax.ShapeDtypeStruct(video.shape, BF16),
        ),
        in_specs=vmem(4),
        out_specs=tuple(vmem(2)),
        cost_estimate=cost(2 * 10**9, 4 * 10**6),
        compiler_params=params(),
        name="prepare",
    )(video, above, below, norm_gain.reshape(1, channels))

    own, windows = lax.optimization_barrier((own, windows))
    other = lax.ppermute(own, "height", [(i, i ^ 1) for i in range(height)])
    core = (lax.axis_index("height") % CORES).astype(jnp.int32).reshape(1)
    places = (rows // 2) * (columns // 2)
    spatial, onward = pl.pallas_call(
        spatial_kernel,
        out_shape=(
            jax.ShapeDtypeStruct(video.shape, BF16),
            jax.ShapeDtypeStruct((places, width), BF16),
        ),
        in_specs=[pl.BlockSpec(memory_space=pltpu.SMEM)] + vmem(5),
        out_specs=tuple(vmem(2)),
        cost_estimate=cost(2 * 10**9, 4 * 10**6),
        compiler_params=params(),
        name="spatial",
    )(core, own, other, windows, temporal_weight, haar_weight)

    carried = lax.ppermute(onward, "tm", [(i, i + 1) for i in range(members - 1)])
    latent = pl.pallas_call(
        latent_kernel,
        out_shape=jax.ShapeDtypeStruct((places, width), F32),
        in_specs=vmem(4),
        out_specs=vmem(1)[0],
        cost_estimate=cost(2 * 10**9, 4 * 10**6),
        compiler_params=params(),
        name="latent",
    )(spatial, ordered, temporal_weight, haar_weight)
    latent = (latent + carried.astype(F32)).astype(BF16)

    per_member = places // members
    sent = latent.reshape(per_member, members, width).transpose(1, 0, 2)
    gathered = lax.all_to_all(sent, "tm", split_axis=0, concat_axis=0, tiled=True)
    encoded = pl.pallas_call(
        attention_kernel,
        out_shape=jax.ShapeDtypeStruct((members, per_member * width), BF16),
        in_specs=vmem(3),
        out_specs=vmem(1)[0],
        cost_estimate=cost(10**9, 4 * 10**6),
        compiler_params=params(),
        name="attention",
    )(gathered.reshape(members, per_member * width), query_weight, key_weight)
    returned = lax.all_to_all(
        encoded.reshape(members, per_member, width), "tm", split_axis=0, concat_axis=0, tiled=True
    )
    return returned.transpose(1, 0, 2).reshape(frames // 2, rows // 2, columns // 2, width)


def solution(mesh):
    in_specs = (
        P(("groups", "tm"), "height", None, None),
        P(),
        P(None, None, "height", None),
        P(),
        P(),
        P(),
        P(),
    )
    out_specs = P(("groups", "tm"), "height", None, None)
    return jax.shard_map(body, mesh=mesh, in_specs=in_specs, out_specs=out_specs, check_vma=False)
```

time: 147 us -> 133 us (0.905)
  blocking collectives: 27.9 us -> 97.9 us
  starting transfers between devices: 58.8 us -> 17.4 us
  waiting for transfers between devices: 42.4 us -> 5.16 us
  other arithmetic: 5.04 us -> 0.01 us
  Pallas kernels: 0 us -> 4.64 us
  matrix products: 4.02 us -> 0 us
    all_to_all x1 -> x2, blocking collectives: 27.9 us -> 97.9 us  [the longest x1 70.1 us: body(): lax.all_to_all(sent, 'tm', split_axis=0, concat_axis=0, tiled=True)]
    all_to_all x2 -> x1, starting transfers between devices: 50.2 us -> 4.58 us  [body(): lax.all_to_all(jnp.broadcast_to(slices, (chips, *slices.shape)), 'height'...]
    all_to_all x2 -> x1, waiting for transfers between devices: 33 us -> 1.67 us  [body(): lax.all_to_all(jnp.broadcast_to(slices, (chips, *slices.shape)), 'height'...]
    ppermute x3 -> x4, waiting for transfers between devices: 9.41 us -> 3.49 us  [the longest x1 1.6 us: body(): other = lax.ppermute(own, 'height', [(i, i ^ 1) for i in range(height)])]
    pallas_call x0 -> x4, Pallas kernels: none -> 4.64 us  [the longest x1 1.68 us: body(): pl.pallas_call(attention_kernel, out_shape=jax.ShapeDtypeStruct((members,...]
    ppermute x3 -> x4, starting transfers between devices: 8.61 us -> 12.8 us  [the longest x1 4.72 us: body(): lax.ppermute(onward, 'tm', [(i, i + 1) for i in range(members - 1)])]
    dot_general x17 -> x0, matrix products: 4.02 us -> none  [the longest x9 2.03 us: body(): jnp.dot(add_window, piece[row_tap, col_tap], preferred_element_type=jnp.f...]
    convert_element_type x3 -> x1, other arithmetic: 2.38 us -> 0.01 us  [body(): latent = (latent + carried.astype(F32)).astype(BF16)]
  transfers between devices with their start and end apart: 5 -> 5, of which waited for: 4 -> 4; matrix products, arithmetic and copies ran while one was open for 3% -> 1% of each run, Pallas kernels for 0% -> 1%
where the time goes in v1:
time: 133 us
  blocking collectives  97.9 us (74%)
  starting transfers between devices  17.4 us (13%)
  local copies, waits for them, and re-layouts  7.57 us (6%)
  waiting for transfers between devices  5.16 us (4%)
  Pallas kernels  4.64 us (3%)
    all_to_all x1, blocking collectives, body(): lax.all_to_all(sent, 'tm', split_axis=0, concat_axis=0, tiled=True)  70.1 us
    all_to_all x1, blocking collectives, body(): lax.all_to_all(encoded.reshape(members, per_member, width), 'tm', split_a...  27.8 us
    ppermute x1, starting transfers between devices, body(): lax.ppermute(onward, 'tm', [(i, i + 1) for i in range(members - 1)])  4.72 us
    all_to_all x1, starting transfers between devices, body(): lax.all_to_all(jnp.broadcast_to(slices, (chips, *slices.shape)), 'height'...  4.58 us
    unnamed x21, local copies, waits for them, and re-layouts  4.07 us
    ppermute x1, starting transfers between devices, body(): other = lax.ppermute(own, 'height', [(i, i ^ 1) for i in range(height)])  3.67 us
    ppermute x1, starting transfers between devices, body(): lax.ppermute(video[:, rows - 1:], 'height', [(i, i + 1) for i in range(he...  3.08 us
  transfers between devices with their start and end apart: 5, of which 4 were waited for; matrix products, arithmetic and copies ran while one was open for 1% of the time, Pallas kernels for 1%

profile of v1, /device:TPU:40, one launch (start us, length us, event | category | flops | bytes accessed | tf_op | source)
XLA Modules:
  0.0 132.7 jit_solution(4115064520173319289)
XLA Ops:
  0.0 1.9 %broadcast_in_dim.3 = bf16[4,9,32,256]{3,2,1,0:T(8,128)(2,1)} broadcast(bf16[9,32,256]{2,1,0:T(8,128)(2,1)} %bitcast.18), dimensions={1,2,3} | broadcast | bytes 737280 | tf_op jit(solution)/shard_map/broadcast_in_dim | solution.py:165
  1.9 4.6 %all-to-all-start = ((bf16[4,9,32,256]{3,2,1,0:T(8,128)(2,1)}), bf16[4,9,32,256]{3,2,1,0:T(8,128)(2,1)S(1)}, u32[]{:S(2)}, u32[]{:S(2)}) async-start(bf16[4,9,32,256]{3,2,1,0:T(8,128)(2,1)} %broadcast_in_dim.3), calls=%async_computation | async-start | bytes 1179648 | tf_op jit(solution)/shard_map/all_to_all | solution.py:164
  6.5 0.9 fusion
  7.3 1.3 collective-permute-start.1
  8.7 3.1 %collective-permute-start = (bf16[2,1,64,256]{3,2,1,0:T(8,128)(2,1)S(1)}, bf16[2,1,64,256]{3,2,1,0:T(8,128)(2,1)S(1)}, u32[]{:S(2)}, u32[]{:S(2)}) collective-permute-start(bf16[2,1,64,256]{3,2,1,0:T(8,128)(2,1)S(1)} %get-tuple-element.18), channel_id=1, source_target_pairs={{0,1},{1,2},{2,3},{3,4},{4,5},{5,6},{6,7},{8,9},{9,10},{10,11},{11... | collective-permute-start | bytes 196616 | tf_op jit(solution)/shard_map/ppermute | solution.py:173
  11.8 0.9 collective-permute-done.above_ref
  12.6 0.6 prepare.1
  13.3 1.0 copy-done.6
  14.3 0.7 copy-done.8
  15.0 1.7 %all-to-all-done.own_ref = bf16[4,9,32,256]{3,2,1,0:T(8,128)(2,1)S(1)} async-done(((bf16[4,9,32,256]{3,2,1,0:T(8,128)(2,1)}), bf16[4,9,32,256]{3,2,1,0:T(8,128)(2,1)S(1)}, u32[]{:S(2)}, u32[]{:S(2)}) %all-to-all-start) | async-done | bytes 589856 | tf_op jit(solution)/shard_map/all_to_all | solution.py:164
  16.7 3.7 %collective-permute-start.2 = (bf16[4,9,32,256]{3,2,1,0:T(8,128)(2,1)S(1)}, bf16[4,9,32,256]{3,2,1,0:T(8,128)(2,1)S(1)}, u32[]{:S(2)}, u32[]{:S(2)}) collective-permute-start(bf16[4,9,32,256]{3,2,1,0:T(8,128)(2,1)S(1)} %all-to-all-done.own_ref), channel_id=1, source_target_pairs={{0,1},{1,0},{2,3},{3,2},{4,5},{5,4},{6,7},{7,6},{8,9},{9,8},{10,11... | collective-permute-start | bytes 1769480 | tf_op jit(solution)/shard_map/ppermute | solution.py:189
  20.4 1.6 %collective-permute-done.2.other_ref = bf16[4,9,32,256]{3,2,1,0:T(8,128)(2,1)S(1)} collective-permute-done((bf16[4,9,32,256]{3,2,1,0:T(8,128)(2,1)S(1)}, bf16[4,9,32,256]{3,2,1,0:T(8,128)(2,1)S(1)}, u32[]{:S(2)}, u32[]{:S(2)}) %collective-permute-start.2) | collective-permute-done | bytes 589856 | tf_op jit(solution)/shard_map/ppermute | solution.py:189
  22.0 1.0 copy-done.4
  23.0 1.3 copy-done.7
  24.3 1.5 %spatial.1 = (bf16[2,4,64,256]{3,2,1,0:T(8,128)(2,1)S(1)}, bf16[64,512]{1,0:T(8,128)(2,1)S(1)}) custom-call(s32[1]{0:T(128)} %bitcast.core_ref, bf16[4,9,32,256]{3,2,1,0:T(8,128)(2,1)S(1)} %all-to-all-done.own_ref, bf16[4,9,32,256]{3,2,1,0:T(8,128)(2,1)S(1)} %collective-permute-done.2.other_ref, bf16[3,2,6,64,256]{4,3,2,1,0:T(8,128)(2,1)S(1)} %copy-done.7, ...), custom_call_target="tpu_custom_call" | custom-call | flops 2000000000 | bytes 4000000 | tf_op jit(solution)/shard_map/spatial/pallas_call | solution.py:192
  25.8 4.7 %collective-permute-start.3 = (bf16[64,512]{1,0:T(8,128)(2,1)S(1)}, bf16[64,512]{1,0:T(8,128)(2,1)S(1)}, u32[]{:S(2)}, u32[]{:S(2)}) collective-permute-start(bf16[64,512]{1,0:T(8,128)(2,1)S(1)} %get-tuple-element.16), channel_id=1, source_target_pairs={{0,8},{8,16},{16,24},{24,32},{32,40},{40,48},{48,56},{56,64},{64,7... | collective-permute-start | bytes 196616 | tf_op jit(solution)/shard_map/ppermute | solution.py:205
  30.5 0.0 copy-start.3
  30.5 0.8 latent.1
  31.4 1.0 collective-permute-done.3
  32.4 0.1 copy.14
  32.5 70.1 %all_to_all.15 = bf16[32,2,512]{2,1,0:T(2,128)(2,1)S(1)} all-to-all(bf16[32,2,512]{2,1,0:T(2,128)(2,1)S(1)} %bitcast.14), channel_id=1, replica_groups=mesh['groups'=2,'tm'=32,'height'=8] {'tm'}, dimensions={0} | all-to-all | bytes 131072 | tf_op jit(solution)/shard_map/all_to_all | solution.py:219
  102.6 1.7 %attention.1 = bf16[32,1024]{1,0:T(8,128)(2,1)S(1)} custom-call(bf16[32,1024]{1,0:T(8,128)(2,1)S(1)} %bitcast.12, bf16[512,512]{1,0:T(8,128)(2,1)S(1)} %copy-done.2, bf16[512,512]{1,0:T(8,128)(2,1)S(1)} %copy-done.3), custom_call_target="tpu_custom_call" | custom-call | flops 1000000000 | bytes 4000000 | tf_op jit(solution)/shard_map/attention/pallas_call | solution.py:220
  104.3 27.8 %all_to_all.16 = bf16[32,2,512]{2,1,0:T(2,128)(2,1)S(1)} all-to-all(bf16[32,2,512]{2,1,0:T(2,128)(2,1)S(1)} %reshape.26), channel_id=1, replica_groups=mesh['groups'=2,'tm'=32,'height'=8] {'tm'}, dimensions={0} | all-to-all | bytes 131072 | tf_op jit(solution)/shard_map/all_to_all | solution.py:229
  132.1 0.6 copy.11
  (19 shorter events, 0.1 us)
Async XLA Ops:
  0.0 12.6 %copy-start = (bf16[2,4,64,256]{3,2,1,0:T(8,128)(2,1)S(1)}, bf16[2,4,64,256]{3,2,1,0:T(8,128)(2,1)}, u32[]{:S(2)}) copy-start(bf16[2,4,64,256]{3,2,1,0:T(8,128)(2,1)} %video_ref.1) | copy-start | bytes 786436
  0.0 12.6 %copy-start.5 = (f32[256]{0:T(256)S(1)}, f32[256]{0:T(256)}, u32[]{:S(2)}) copy-start(f32[256]{0:T(256)} %param.8) | copy-start | bytes 3076
  1.9 14.8 %all-to-all-start = ((bf16[4,9,32,256]{3,2,1,0:T(8,128)(2,1)}), bf16[4,9,32,256]{3,2,1,0:T(8,128)(2,1)S(1)}, u32[]{:S(2)}, u32[]{:S(2)}) async-start(bf16[4,9,32,256]{3,2,1,0:T(8,128)(2,1)} %broadcast_in_dim.3), calls=%async_computation | async-start | bytes 1179648 | tf_op jit(solution)/shard_map/all_to_all | solution.py:164
  7.3 4.4 %collective-permute-start.1 = (bf16[2,1,64,256]{3,2,1,0:T(8,128)(2,1)S(1)}, bf16[2,1,64,256]{3,2,1,0:T(8,128)(2,1)S(1)}, u32[]{:S(2)}, u32[]{:S(2)}) collective-permute-start(bf16[2,1,64,256]{3,2,1,0:T(8,128)(2,1)S(1)} %get-tuple-element.17), channel_id=1, source_target_pairs={{1,0},{2,1},{3,2},{4,3},{5,4},{6,5},{7,6},{9,8},{10,9},{11,10},{12... | collective-permute-start | bytes 196616 | tf_op jit(solution)/shard_map/ppermute | solution.py:174
  8.7 4.0 %collective-permute-start = (bf16[2,1,64,256]{3,2,1,0:T(8,128)(2,1)S(1)}, bf16[2,1,64,256]{3,2,1,0:T(8,128)(2,1)S(1)}, u32[]{:S(2)}, u32[]{:S(2)}) collective-permute-start(bf16[2,1,64,256]{3,2,1,0:T(8,128)(2,1)S(1)} %get-tuple-element.18), channel_id=1, source_target_pairs={{0,1},{1,2},{2,3},{3,4},{4,5},{5,6},{6,7},{8,9},{9,10},{10,11},{11... | collective-permute-start | bytes 196616 | tf_op jit(solution)/shard_map/ppermute | solution.py:173
  12.6 9.4 %copy-start.1 = (bf16[2048,512]{1,0:T(8,128)(2,1)S(1)}, bf16[2048,512]{1,0:T(8,128)(2,1)}, u32[]{:S(2)}) copy-start(bf16[2048,512]{1,0:T(8,128)(2,1)} %haar_ref.3) | copy-start | bytes 6291460
  13.3 1.1 copy-start.6
  14.3 0.7 copy-start.8
  16.7 5.3 %collective-permute-start.2 = (bf16[4,9,32,256]{3,2,1,0:T(8,128)(2,1)S(1)}, bf16[4,9,32,256]{3,2,1,0:T(8,128)(2,1)S(1)}, u32[]{:S(2)}, u32[]{:S(2)}) collective-permute-start(bf16[4,9,32,256]{3,2,1,0:T(8,128)(2,1)S(1)} %all-to-all-done.own_ref), channel_id=1, source_target_pairs={{0,1},{1,0},{2,3},{3,2},{4,5},{5,4},{6,7},{7,6},{8,9},{9,8},{10,11... | collective-permute-start | bytes 1769480 | tf_op jit(solution)/shard_map/ppermute | solution.py:189
  22.0 1.0 copy-start.4
  23.0 1.3 copy-start.7
  24.3 6.2 %copy-start.9 = (bf16[2,4,64,256]{3,2,1,0:T(8,128)(2,1)S(1)}, bf16[2,4,64,256]{3,2,1,0:T(8,128)(2,1)}, u32[]{:S(2)}) copy-start(bf16[2,4,64,256]{3,2,1,0:T(8,128)(2,1)} %copy-done.8) | copy-start | bytes 786436
  25.8 6.6 %collective-permute-start.3 = (bf16[64,512]{1,0:T(8,128)(2,1)S(1)}, bf16[64,512]{1,0:T(8,128)(2,1)S(1)}, u32[]{:S(2)}, u32[]{:S(2)}) collective-permute-start(bf16[64,512]{1,0:T(8,128)(2,1)S(1)} %get-tuple-element.16), channel_id=1, source_target_pairs={{0,8},{8,16},{16,24},{24,32},{32,40},{40,48},{48,56},{56,64},{64,7... | collective-permute-start | bytes 196616 | tf_op jit(solution)/shard_map/ppermute | solution.py:205
  30.5 72.1 %copy-start.2 = (bf16[512,512]{1,0:T(8,128)(2,1)S(1)}, bf16[512,512]{1,0:T(8,128)(2,1)}, u32[]{:S(2)}) copy-start(bf16[512,512]{1,0:T(8,128)(2,1)} %query_ref.1) | copy-start | bytes 1572868
  30.5 72.1 %copy-start.3 = (bf16[512,512]{1,0:T(8,128)(2,1)S(1)}, bf16[512,512]{1,0:T(8,128)(2,1)}, u32[]{:S(2)}) copy-start(bf16[512,512]{1,0:T(8,128)(2,1)} %key_ref.1) | copy-start | bytes 1572868
